TPU v7x, 256 devices: a whole 4x4x8 slice. The times are simulated.
256 devices in a mesh: rows: 32 (over y, x, core), cols: 8 (over z).
Axes of the slice: x: 4, y: 4, z: 8, core: 2. Of those that a mesh axis runs over, the one named last changes fastest.
Arguments:
- one_query: float32 [8192, 8192], P('rows', 'cols'), may hold values from -0.125 to 0.125
- other_query: float32 [8192, 8192], P('rows', 'cols'), may hold values from -0.0625 to 0.0625
- one_key: float32 [8192, 512], P('rows', 'cols'), may hold values from -0.125 to 0.125
- other_key: float32 [8192, 512], P('rows', 'cols'), may hold values from -0.0625 to 0.0625
- one_value: float32 [8192, 512], P('rows', 'cols'), may hold values from -0.125 to 0.125
- other_value: float32 [8192, 512], P('rows', 'cols'), may hold values from -0.0625 to 0.0625
- mix_share: float32 [8192], P('rows'), may hold values from 0.2 to 0.8
- norm_gain: float32 [8192], P('rows'), may hold values from 0.25 to 1.75
Outputs:
- serve_query: bfloat16 [8192, 8192], P(None, 'cols')
- serve_key: bfloat16 [8192, 512], P(None, 'cols')
- serve_value: bfloat16 [8192, 512], P(None, 'cols')
- scale_query: float32 [8192], P('cols')
- scale_key: float32 [512], P('cols')
- scale_value: float32 [512], P('cols')
All inputs are finite; a program needn't handle non-finite values. Where the computation divides by a largest or mean magnitude, that divisor is 1e-20 or more.
Results may differ from a plain program's by a relative error of at most 0.001.
Values may be sent and summed in bfloat16 or wider, within the bound.
A program may use at most 128 MiB of HBM per device.

v0:
```python
import functools
import math

import jax
import jax.numpy as jnp
from jax import lax
from jax.experimental import pallas as pl
from jax.experimental.pallas import tpu as pltpu
from jax.sharding import PartitionSpec as P

MESH = pl.DeviceIdType.MESH
CHUNK = 256
STEP_ROWS = 64


def ring_of(chips):
    side = math.isqrt(chips)
    if side * side != chips or side % 2 or side < 2:
        return list(range(chips))
    cycle = [y * side for y in range(side)]
    for k in range(side):
        y = side - 1 - k
        xs = range(1, side) if k % 2 == 0 else range(side - 1, 0, -1)
        cycle += [y * side + x for x in xs]
    return cycle


def pick(table, index):
    out = jnp.int32(table[0])
    for at in range(1, len(table)):
        out = jnp.where(index == at, jnp.int32(table[at]), out)
    return out


def kernel(
    ranks, d_model, plan,
    share_ref, rest_ref, oq, tq, ok, tk, ov, tv,
    sq, sk, sv, cq, ck, cv,
    one_wide, other_wide, narrow_wide, mine_wide, sums_wide,
    one_slim, other_slim, narrow_slim, mine_slim, sums_slim,
    in_sem, stat_send, stat_recv, own_sem, ring_send, ring_recv, twin_send, twin_recv,
):
    me = lax.axis_index("rows")
    chips = ranks // 2
    chip, core = me // 2, me % 2
    cycle = ring_of(chips)
    place = [cycle.index(c) for c in range(chips)]
    spot = pick(place, chip)
    ahead = pick([cycle[(place[c] + 1) % chips] for c in range(chips)], chip)
    behind = pick([cycle[(place[c] - 1) % chips] for c in range(chips)], chip)
    next_dev = (ahead * 2 + core, behind * 2 + core)
    twin = chip * 2 + 1 - core
    rows = oq.shape[0]
    half = rows // 2
    steps = chips // 2
    firsts, others = (oq, ok, ov), (tq, tk, tv)
    outs, scales = (sq, sk, sv), (cq, ck, cv)

    one, other, narrow, mine, sums = {}, {}, {}, {}, {}
    for j, (which, slot, col, width) in enumerate(plan):
        slim = which > 0
        one[j] = (one_slim if slim else one_wide).at[slot]
        other[j] = (other_slim if slim else other_wide).at[slot]
        narrow[j] = (narrow_slim if slim else narrow_wide).at[slot]
        mine[j] = (mine_slim if slim else mine_wide).at[slot]
        for shift in range(1, ranks):
            sums[shift, j] = (sums_slim if slim else sums_wide).at[shift, slot]

    def window(ref, j, first, count):
        which, slot, col, width = plan[j]
        if which > 0:
            return ref.at[pl.ds(first, count)]
        return ref.at[pl.ds(first, count), pl.ds(col, width)]

    def origin(way, step):
        at = lax.rem(spot - step + chips, chips) if way == 0 else lax.rem(spot + step, chips)
        return pick(cycle, at) * 2 + core

    def span(way, step):
        if chips % 2 == 0 and step == steps:
            return way * half, half
        return 0, rows

    loads = []
    for j, (which, slot, col, width) in enumerate(plan):
        pair = []
        for k, (source, held) in enumerate(((firsts, one), (others, other))):
            copy = pltpu.make_async_copy(
                window(source[which], j, 0, rows),
                held[j],
                in_sem.at[k, j],
            )
            copy.start()
            pair.append(copy)
        loads.append(pair)

    barrier = pltpu.get_barrier_semaphore()
    for shift in range(1, ranks):
        pl.semaphore_signal(
            barrier, inc=1, device_id={"rows": lax.rem(me + shift, ranks)}, device_id_type=MESH
        )

    stat_copies = {}
    pending = []

    def tiles(width):
        return [(c, min(128, width - c)) for c in range(0, width, 128)]

    def measure(j):
        which, slot, col, width = plan[j]
        loads[j][0].wait()
        loads[j][1].wait()
        cuts = tiles(width)

        def body(i, accs):
            r = pl.ds(pl.multiple_of(i * STEP_ROWS, STEP_ROWS), STEP_ROWS)
            new = []
            for (c, w), acc in zip(cuts, accs):
                a, b = share_ref[r, pl.ds(0, w)], rest_ref[r, pl.ds(0, w)]
                f = a * one[j][r, pl.ds(c, w)] + b * other[j][r, pl.ds(c, w)]
                one[j][r, pl.ds(c, w)] = f
                new.append(acc + jnp.sum(jnp.abs(f).reshape(STEP_ROWS // 8, 8, w), axis=0))
            return tuple(new)

        accs = lax.fori_loop(
            0, rows // STEP_ROWS, body, tuple(jnp.zeros((8, w), jnp.float32) for _, w in cuts)
        )
        for (c, w), acc in zip(cuts, accs):
            mine[j][:, pl.ds(c, w)] = jnp.sum(acc, axis=0, keepdims=True)

    def share(j):
        if j == 0:
            pl.semaphore_wait(barrier, ranks - 1)
        for shift in range(1, ranks):
            copy = pltpu.make_async_remote_copy(
                src_ref=mine[j],
                dst_ref=sums[shift, j],
                send_sem=stat_send.at[shift, j],
                recv_sem=stat_recv.at[shift, j],
                device_id={"rows": lax.rem(me + shift, ranks)},
                device_id_type=MESH,
            )
            copy.start()
            stat_copies[shift, j] = copy

    def remote(src, dst, send, recv, device):
        copy = pltpu.make_async_remote_copy(
            src_ref=src, dst_ref=dst, send_sem=send, recv_sem=recv,
            device_id={"rows": device}, device_id_type=MESH,
        )
        copy.start()
        return copy

    def block(j, dev, first, count):
        which, slot, col, width = plan[j]
        start = pl.multiple_of(dev * rows + first, half)
        return window(outs[which], j, start, count)

    ring = {}
    twins = {}

    def finish(j):
        which, slot, col, width = plan[j]
        for shift in range(1, ranks):
            stat_copies[shift, j].wait()
        inverses = []
        for c, w in tiles(width):
            total = jnp.zeros((1, w), jnp.float32)
            for owner in range(ranks):
                part = mine[j][:, pl.ds(c, w)]
                for shift in range(1, ranks):
                    sent = sums[shift, j][:, pl.ds(c, w)]
                    part = jnp.where(lax.rem(me - owner + ranks, ranks) == shift, sent, part)
                total = total + part
            scale = total / d_model
            scales[which][:, pl.ds(col + c, w)] = scale
            inverses.append(1.0 / scale)

        def body(i, carry):
            r = pl.ds(pl.multiple_of(i * STEP_ROWS, STEP_ROWS), STEP_ROWS)
            for (c, w), inverse in zip(tiles(width), inverses):
                narrow[j][r, pl.ds(c, w)] = (one[j][r, pl.ds(c, w)] * inverse).astype(jnp.bfloat16)
            return carry

        lax.fori_loop(0, rows // STEP_ROWS, body, 0)

    def send(j):
        which, slot, col, width = plan[j]
        for way in range(2):
            if steps:
                first, count = span(way, 1)
                ring[way, 1, j] = remote(
                    narrow[j].at[pl.ds(first, count)],
                    block(j, me, first, count),
                    ring_send.at[way, 0, j], ring_recv.at[way, 0, j], next_dev[way],
                )
        twins[0, 0, j] = remote(
            narrow[j], block(j, me, 0, rows),
            twin_send.at[0, 0, j], twin_recv.at[0, 0, j], twin,
        )
        copy = pltpu.make_async_copy(
            narrow[j], block(j, me, 0, rows), own_sem.at[j]
        )
        copy.start()
        pending.append(copy)

    count = len(plan)
    measure(0)
    share(0)
    for j in range(count):
        if j + 1 < count:
            measure(j + 1)
            share(j + 1)
        finish(j)
        send(j)

    for step in range(1, steps + 1):
        for j in range(count):
            for way in range(2):
                ring[way, step, j].wait_recv()
                dev = origin(way, step)
                if step < steps:
                    first, n = span(way, step + 1)
                    piece = block(j, dev, first, n)
                    ring[way, step + 1, j] = remote(
                        piece, piece,
                        ring_send.at[way, step, j], ring_recv.at[way, step, j], next_dev[way],
                    )
                first, n = span(way, step)
                piece = block(j, dev, first, n)
                twins[way, step, j] = remote(
                    piece, piece,
                    twin_send.at[way, step, j], twin_recv.at[way, step, j], twin,
                )
    for copy in pending:
        copy.wait()
    for copy in ring.values():
        copy.wait_send()
    for copy in twins.values():
        copy.wait()


def local(ranks, d_model, one_query, other_query, one_key, other_key, one_value, other_value, mix_share, norm_gain):
    rows, q_cols = one_query.shape
    kv_cols = one_key.shape[1]
    width = min(CHUNK, q_cols)
    plan = [(0, col // width, col, width) for col in range(0, q_cols, width)]
    plan += [(1, 0, 0, kv_cols), (2, 1, 0, kv_cols)]
    scratch = []
    for slots, wide in ((q_cols // width, width), (2, kv_cols)):
        scratch += [
            pltpu.VMEM((slots, rows, wide), jnp.float32),
            pltpu.VMEM((slots, rows, wide), jnp.float32),
            pltpu.VMEM((slots, rows, wide), jnp.bfloat16),
            pltpu.VMEM((slots, 1, wide), jnp.float32),
            pltpu.VMEM((ranks, slots, 1, wide), jnp.float32),
        ]
    count = len(plan)
    steps = ranks // 4
    share = jnp.broadcast_to((norm_gain * mix_share)[:, None], (rows, 128))
    rest = jnp.broadcast_to((norm_gain * (1.0 - mix_share))[:, None], (rows, 128))
    whole = ranks * rows
    vmem = pl.BlockSpec(memory_space=pltpu.VMEM)
    hbm = pl.BlockSpec(memory_space=pl.ANY)
    dma = pltpu.SemaphoreType.DMA
    sq, sk, sv, cq, ck, cv = pl.pallas_call(
        functools.partial(kernel, ranks, d_model, plan),
        out_shape=(
            jax.ShapeDtypeStruct((whole, q_cols), jnp.bfloat16),
            jax.ShapeDtypeStruct((whole, kv_cols), jnp.bfloat16),
            jax.ShapeDtypeStruct((whole, kv_cols), jnp.bfloat16),
            jax.ShapeDtypeStruct((1, q_cols), jnp.float32),
            jax.ShapeDtypeStruct((1, kv_cols), jnp.float32),
            jax.ShapeDtypeStruct((1, kv_cols), jnp.float32),
        ),
        in_specs=[vmem, vmem] + [hbm] * 6,
        out_specs=(hbm, hbm, hbm, vmem, vmem, vmem),
        scratch_shapes=scratch
        + [
            dma((2, count)),
            dma((ranks, count)),
            dma((ranks, count)),
            dma((count,)),
            dma((2, max(steps, 1), count)),
            dma((2, max(steps, 1), count)),
            dma((2, steps + 1, count)),
            dma((2, steps + 1, count)),
        ],
        compiler_params=pltpu.CompilerParams(
            collective_id=0, has_side_effects=True, vmem_limit_bytes=50 * 1024 * 1024
        ),
    )(share, rest, one_query, other_query, one_key, other_key, one_value, other_value)
    return sq, sk, sv, cq[0], ck[0], cv[0]


def solution(mesh):
    def body(one_query, *rest):
        ranks = mesh.shape["rows"]
        return local(ranks, ranks * one_query.shape[0], one_query, *rest)

    return jax.shard_map(
        body,
        mesh=mesh,
        in_specs=(P("rows", "cols"),) * 6 + (P("rows"),) * 2,
        out_specs=(P(None, "cols"),) * 3 + (P("cols"),) * 3,
        check_vma=False,
    )
```

profile of v0, /device:TPU:1, one launch (start us, length us, event | category | flops | bytes accessed | tf_op | source)
XLA Modules:
  0.0 163.0 jit_solution(9690131451541905575)
XLA Ops:
  0.6 0.7 subtract_multiply_fusion
  1.3 0.1 broadcast_in_dim.5.rest_ref
  1.4 0.1 broadcast_in_dim.4.share_ref
  1.5 0.9 copy.14.ok
  2.5 0.9 copy.15.tk
  3.4 0.9 copy.16.ov
  4.3 0.9 copy.17.tv
  5.3 0.0 copy-start
  5.3 1.2 copy-done
  6.5 0.0 copy-start.1
  6.5 1.2 copy-done.1
  7.7 134.3 %shard_map.127 = (bf16[8192,1024]{1,0:T(8,128)(2,1)}, bf16[8192,64]{1,0:T(8,128)(2,1)}, bf16[8192,64]{1,0:T(8,128)(2,1)}, f32[1,1024]{1,0:T(1,128)S(1)}, f32[1,64]{1,0:T(1,128)S(1)}, /*index=5*/f32[1,64]{1,0:T(1,128)S(1)}) custom-call(f32[256,128]{1,0:T(8,128)S(1)} %broadcast_in_dim.4.share_ref, f32[256,128]{1,0:T(8,128)S(1)} %broadcast_in_dim.5.rest_ref, ...), custom_call_target="tpu_custom_call" | custom-call | tf_op jit(solution)/shard_map/pallas_call | solution.py:266
  142.1 2.7 %copy.18 = bf16[8192,64]{0,1:T(8,128)(2,1)} copy(bf16[8192,64]{1,0:T(8,128)(2,1)} %get-tuple-element.19) | data formatting | bytes 2097152
  144.8 2.7 %copy.19 = bf16[8192,64]{0,1:T(8,128)(2,1)} copy(bf16[8192,64]{1,0:T(8,128)(2,1)} %get-tuple-element.20) | data formatting | bytes 2097152
  147.4 13.9 %copy.24 = bf16[8192,1024]{1,0:T(8,128)(2,1)} copy(bf16[8192,1024]{1,0:T(8,128)(2,1)} %get-tuple-element.32) | data formatting | bytes 33554432
  161.4 0.6 copy.25
  161.9 0.5 copy.26
  162.5 0.5 copy.27
Async XLA Ops:
  5.3 1.2 copy-start
  6.5 1.2 copy-start.1
where the time goes:
time: 163 us
  Pallas kernels  134 us (82%)
  local copies, waits for them, and re-layouts  27.3 us (17%)
    pallas_call x1, Pallas kernels, local(): pl.pallas_call(functools.partial(kernel, ranks, d_model, plan), out_shape...  134 us
    unnamed x14, local copies, waits for them, and re-layouts  27.1 us

commit v1 on v0

v1 whole, which is shorter than its diff:
```python
import functools
import math

import jax
import jax.numpy as jnp
from jax import lax
from jax.experimental import pallas as pl
from jax.experimental.pallas import tpu as pltpu
from jax.sharding import PartitionSpec as P

MESH = pl.DeviceIdType.MESH
CHUNKS = 2
SLABS = 4
STEP_ROWS = 32


def chip_at(cycle, place, side):
    major = lax.div(place, side)
    minor = lax.rem(place - major + side, side)
    y, x = (minor, major) if cycle == 0 else (major, minor)
    return y * side + x


def place_of(cycle, chip, side):
    y, x = lax.div(chip, side), lax.rem(chip, side)
    major, minor = (x, y) if cycle == 0 else (y, x)
    return major * side + lax.rem(minor + major, side)


def gather_kernel(
    ranks, d_model,
    mix_hbm, gain_hbm, oq, tq, ok, tk, ov, tv,
    sq, sk, sv, cq, ck, cv,
    mix, gain, one, other, one_kv, other_kv, col_a, col_b, sums,
    coef_sem, q_sem, kv_sem, stat_send, stat_recv, ring_send, ring_recv,
    own_send, own_recv, twin_send, twin_recv,
):
    me = lax.axis_index("rows")
    chips = ranks // 2
    side = math.isqrt(chips)
    steps = chips // 2
    chip, core = lax.div(me, 2), lax.rem(me, 2)
    twin = chip * 2 + 1 - core
    rows, q_cols = oq.shape
    kv_cols = ok.shape[0]
    half = rows // 2
    chunk = half // CHUNKS
    slab = rows // SLABS
    tiles = q_cols // 128

    loads = []
    for n, (source, held) in enumerate(((mix_hbm, mix), (gain_hbm, gain))):
        copy = pltpu.make_async_copy(source, held, coef_sem.at[n])
        copy.start()
        loads.append(copy)
    q_loads = []
    for s in range(SLABS):
        r = pl.ds(s * slab, slab)
        pair = []
        for n, (source, held) in enumerate(((oq, one), (tq, other))):
            copy = pltpu.make_async_copy(source.at[r], held.at[r], q_sem.at[n, s])
            copy.start()
            pair.append(copy)
        q_loads.append(pair)
    kv_loads = []
    for n, (source, held) in enumerate(
        ((ok, one_kv.at[pl.ds(0, kv_cols)]), (tk, other_kv.at[pl.ds(0, kv_cols)]),
         (ov, one_kv.at[pl.ds(kv_cols, kv_cols)]), (tv, other_kv.at[pl.ds(kv_cols, kv_cols)]))
    ):
        copy = pltpu.make_async_copy(source, held, kv_sem.at[n])
        copy.start()
        kv_loads.append(copy)

    barrier = pltpu.get_barrier_semaphore()
    for shift in range(1, ranks):
        pl.semaphore_signal(
            barrier, inc=1, device_id={"rows": lax.rem(me + shift, ranks)}, device_id_type=MESH
        )

    for copy in loads:
        copy.wait()
    a_row = gain[...] * mix[...]
    b_row = gain[...] * (1.0 - mix[...])
    for c in range(0, rows, 128):
        col_a[pl.ds(c, 128), :] = jnp.broadcast_to(a_row[:, c:c + 128], (128, 128)).T
        col_b[pl.ds(c, 128), :] = jnp.broadcast_to(b_row[:, c:c + 128], (128, 128)).T

    accs = tuple(jnp.zeros((8, 128), jnp.float32) for _ in range(tiles))
    for s in range(SLABS):
        for copy in q_loads[s]:
            copy.wait()

        def body(i, accs):
            r = pl.ds(pl.multiple_of(s * slab + i * STEP_ROWS, STEP_ROWS), STEP_ROWS)
            a, b = col_a[r, :], col_b[r, :]
            new = []
            for j, acc in enumerate(accs):
                c = pl.ds(j * 128, 128)
                f = a * one[r, c] + b * other[r, c]
                one[r, c] = f
                new.append(acc + jnp.sum(jnp.abs(f).reshape(STEP_ROWS // 8, 8, 128), axis=0))
            return tuple(new)

        accs = lax.fori_loop(0, slab // STEP_ROWS, body, accs)
    for j, acc in enumerate(accs):
        sums[me, pl.ds(j, 1), :] = jnp.sum(acc, axis=0, keepdims=True)
    for copy in kv_loads:
        copy.wait()
    f = a_row * one_kv[...] + b_row * other_kv[...]
    one_kv[...] = f
    sizes = jnp.abs(f)
    size = sizes[:, 0:128]
    for c in range(128, rows, 128):
        size = size + sizes[:, c:c + 128]
    sums[me, pl.ds(tiles, 1), :] = jnp.sum(size.T, axis=0, keepdims=True)

    def remote(src, dst, send, recv, device):
        copy = pltpu.make_async_remote_copy(
            src_ref=src, dst_ref=dst, send_sem=send, recv_sem=recv,
            device_id={"rows": device}, device_id_type=MESH,
        )
        copy.start()
        return copy

    pl.semaphore_wait(barrier, ranks - 1)
    stats = []
    for shift in range(1, ranks):
        place = sums.at[me]
        stats.append(remote(
            place, place, stat_send.at[shift], stat_recv.at[shift], lax.rem(me + shift, ranks)
        ))

    spots = [place_of(c, chip, side) for c in range(2)]
    aims = {}
    for c in range(2):
        aims[c, 0] = chip_at(c, lax.rem(spots[c] + 1, chips), side) * 2 + core
        aims[c, 1] = chip_at(c, lax.rem(spots[c] + chips - 1, chips), side) * 2 + core

    for copy in stats:
        copy.wait_recv()
    total = sums[0, 0:tiles + 1, :]
    for owner in range(1, ranks):
        total = total + sums[owner, 0:tiles + 1, :]
    scale = total / d_model
    inverse = 1.0 / scale

    def piece(c, dev, n, way=None):
        if n < CHUNKS:
            at = pl.multiple_of(dev * rows + c * half + n * chunk, chunk)
            return sq.at[pl.ds(at, chunk)]
        ref = (sk, sv)[c]
        at = pl.ds(pl.multiple_of(dev * rows, rows), rows)
        if way is None:
            return ref.at[:, at]
        return ref.at[pl.ds(way * (kv_cols // 2), kv_cols // 2), at]

    def parts(step, way):
        if step < steps:
            return list(range(CHUNKS + 1))
        return list(range(way * CHUNKS // 2, (way + 1) * CHUNKS // 2)) + [CHUNKS]

    ring = {}
    twins = {}

    def launch(c, way, step, n, dev):
        spot = piece(c, dev, n, way if step == steps else None)
        ring[c, way, step, n] = remote(
            spot, spot, ring_send.at[c, way, step - 1, n], ring_recv.at[c, way, step - 1, n],
            aims[c, way],
        )

    for n in range(CHUNKS):
        for c in range(2):
            def body(i, carry, c=c, n=n):
                first = c * half + n * chunk + i * STEP_ROWS
                r = pl.ds(pl.multiple_of(first, STEP_ROWS), STEP_ROWS)
                to = pl.ds(pl.multiple_of(me * rows + first, STEP_ROWS), STEP_ROWS)
                for j in range(tiles):
                    col = pl.ds(j * 128, 128)
                    sq[to, col] = (one[r, col] * inverse[j:j + 1, :]).astype(jnp.bfloat16)
                return carry

            lax.fori_loop(0, chunk // STEP_ROWS, body, 0)
            for way in range(2):
                launch(c, way, 1, n, me)
    flip = jnp.broadcast_to(inverse[tiles:tiles + 1, :], (128, 128)).T
    own = pl.multiple_of(me * rows, rows)
    for c, ref in enumerate((sk, sv)):
        r = pl.ds(c * kv_cols, kv_cols)
        for col in range(0, rows, 128):
            ref[:, pl.ds(pl.multiple_of(own + col, 128), 128)] = (
                one_kv[r, pl.ds(col, 128)] * flip[c * kv_cols:(c + 1) * kv_cols, :]
            ).astype(jnp.bfloat16)
        for way in range(2):
            launch(c, way, 1, CHUNKS, me)
    for c in range(2):
        for n in range(CHUNKS + 1):
            spot = piece(c, me, n)
            twins[c, n] = remote(spot, spot, own_send.at[c, n], own_recv.at[c, n], twin)

    for j in range(tiles):
        cq[:, pl.ds(j * 128, 128)] = scale[j:j + 1, :]
    ck[...] = scale[tiles:tiles + 1, 0:kv_cols]
    cv[...] = scale[tiles:tiles + 1, kv_cols:2 * kv_cols]

    for step in range(1, steps + 1):
        devs = {}
        for c in range(2):
            devs[c, 0] = chip_at(c, lax.rem(spots[c] + chips - step, chips), side) * 2 + core
            devs[c, 1] = chip_at(c, lax.rem(spots[c] + step, chips), side) * 2 + core
        for n in range(CHUNKS + 1):
            for c in range(2):
                for way in range(2):
                    if n not in parts(step, way):
                        continue
                    ring[c, way, step, n].wait_recv()
                    if step < steps and n in parts(step + 1, way):
                        launch(c, way, step + 1, n, devs[c, way])
                    spot = piece(c, devs[c, way], n, way if step == steps else None)
                    twins[c, way, step, n] = remote(
                        spot, spot, twin_send.at[c, way, step - 1, n],
                        twin_recv.at[c, way, step - 1, n], twin,
                    )
    for copy in stats:
        copy.wait_send()
    for copy in ring.values():
        copy.wait_send()
    for copy in twins.values():
        copy.wait()


def write_kernel(sq, sk, sv, cq, ck, cv, oq, ok, ov, dq, dk, dv, q_sem, sem):
    count = q_sem.shape[0]
    rows = sq.shape[0] // count
    copies = []
    for n in range(count):
        r = pl.ds(n * rows, rows)
        copies.append(pltpu.make_async_copy(sq.at[r], oq.at[r], q_sem.at[n]))
    for n, (source, out) in enumerate(((sk, ok), (sv, ov), (cq, dq), (ck, dk), (cv, dv))):
        copies.append(pltpu.make_async_copy(source, out, sem.at[n]))
    for copy in copies:
        copy.start()
    for copy in copies:
        copy.wait()


def local(ranks, d_model, one_query, other_query, one_key, other_key, one_value, other_value, mix_share, norm_gain):
    rows, q_cols = one_query.shape
    kv_cols = one_key.shape[1]
    whole = ranks * rows
    steps = ranks // 4
    vmem = pl.BlockSpec(memory_space=pltpu.VMEM)
    hbm = pl.BlockSpec(memory_space=pltpu.HBM)
    dma = pltpu.SemaphoreType.DMA
    f32, bf16 = jnp.float32, jnp.bfloat16
    shapes = (
        jax.ShapeDtypeStruct((whole, q_cols), bf16),
        jax.ShapeDtypeStruct((kv_cols, whole), bf16),
        jax.ShapeDtypeStruct((kv_cols, whole), bf16),
        jax.ShapeDtypeStruct((1, q_cols), f32),
        jax.ShapeDtypeStruct((1, kv_cols), f32),
        jax.ShapeDtypeStruct((1, kv_cols), f32),
    )
    pieces = CHUNKS + 1
    landed = pl.pallas_call(
        functools.partial(gather_kernel, ranks, d_model),
        out_shape=tuple(pltpu.VMEM(x.shape, x.dtype) for x in shapes),
        in_specs=[hbm] * 8,
        out_specs=(vmem,) * 6,
        scratch_shapes=[
            pltpu.VMEM((1, rows), f32),
            pltpu.VMEM((1, rows), f32),
            pltpu.VMEM((rows, q_cols), f32),
            pltpu.VMEM((rows, q_cols), f32),
            pltpu.VMEM((2 * kv_cols, rows), f32),
            pltpu.VMEM((2 * kv_cols, rows), f32),
            pltpu.VMEM((rows, 128), f32),
            pltpu.VMEM((rows, 128), f32),
            pltpu.VMEM((ranks, 16, 128), f32),
            dma((2,)),
            dma((2, SLABS)),
            dma((4,)),
            dma((ranks,)),
            dma((ranks,)),
            dma((2, 2, steps, pieces)),
            dma((2, 2, steps, pieces)),
            dma((2, pieces)),
            dma((2, pieces)),
            dma((2, 2, steps, pieces)),
            dma((2, 2, steps, pieces)),
        ],
        compiler_params=pltpu.CompilerParams(
            collective_id=0, has_side_effects=True, vmem_limit_bytes=VMEM_A
        ),
    )(*(
        pltpu.with_memory_space_constraint(x, pltpu.HBM)
        for x in (
            mix_share.reshape(1, rows), norm_gain.reshape(1, rows), one_query, other_query,
            one_key.T, other_key.T, one_value.T, other_value.T,
        )
    ))
    out = pl.pallas_call(
        write_kernel,
        out_shape=shapes,
        in_specs=[vmem] * 6,
        out_specs=(hbm,) * 6,
        scratch_shapes=[dma((8,)), dma((5,))],
        compiler_params=pltpu.CompilerParams(vmem_limit_bytes=VMEM_B),
    )(*landed)
    sq, sk, sv, cq, ck, cv = out
    return sq, sk.T, sv.T, cq[0], ck[0], cv[0]


VMEM_A = 10 * 1024 * 1024
VMEM_B = 2 * 1024 * 1024


def solution(mesh):
    def body(one_query, *rest):
        ranks = mesh.shape["rows"]
        return local(ranks, ranks * one_query.shape[0], one_query, *rest)

    return jax.shard_map(
        body,
        mesh=mesh,
        in_specs=(P("rows", "cols"),) * 6 + (P("rows"),) * 2,
        out_specs=(P(None, "cols"),) * 3 + (P("cols"),) * 3,
        check_vma=False,
    )
```

time: 163 us -> 77.1 us (0.47)
  Pallas kernels: 134 us -> 76.3 us
  local copies, waits for them, and re-layouts: 27.3 us -> 0 us
    pallas_call x1 -> x2, Pallas kernels: 134 us -> 76.3 us  [the longest x1 69.7 us: local(): pl.pallas_call(functools.partial(gather_kernel, ranks, d_model), out_shap...]
    unnamed x14 -> x0, local copies, waits for them, and re-layouts: 27.1 us -> none
where the time goes in v1:
time: 77.1 us; the launch traced here: 76.9 us
  Pallas kernels  76.3 us (99%)
    pallas_call x1, Pallas kernels, local(): pl.pallas_call(functools.partial(gather_kernel, ranks, d_model), out_shap...  69.7 us
    pallas_call x1, Pallas kernels, local(): pl.pallas_call(write_kernel, out_shape=shapes, in_specs=[vmem] * 6, out_s...  6.62 us

profile of v1, /device:TPU:1, one launch (start us, length us, event | category | flops | bytes accessed | tf_op | source)
XLA Modules:
  0.0 76.9 jit_solution(4273357359933223598)
XLA Ops:
  0.6 69.7 %shard_map.127 = (bf16[8192,1024]{1,0:T(8,128)(2,1)S(1)}, bf16[64,8192]{1,0:T(8,128)(2,1)S(1)}, bf16[64,8192]{1,0:T(8,128)(2,1)S(1)}, f32[1,1024]{1,0:T(1,128)S(...) custom-call(f32[1,256]{1,0:T(1,128)} %bitcast.15, f32[1,256]{1,0:T(1,128)} %bitcast.16, f32[256,1024]{1,0:T(8,128)} %oq.1, ...), custom_call_target="tpu_custom_call" | custom-call | tf_op jit(solution)/shard_map/pallas_call | solution.py:265
  70.3 6.6 %shard_map.128 = (bf16[8192,1024]{1,0:T(8,128)(2,1)}, bf16[64,8192]{1,0:T(8,128)(2,1)}, bf16[64,8192]{1,0:T(8,128)(2,1)}, f32[1,1024]{1,0:T(1,128)}, f32[1,64]{1,0:T(1,128)}, /*index=5*/f32[1,64]{1,0:T(1,128)}) custom-call(bf16[8192,1024]{1,0:T(8,128)(2,1)S(1)} %get-tuple-element.18.sq, bf16[64,8192]{1,0:T(8,128)(2,1)S(1)} %get-tuple-element.19.sk, ...), custom_call_target="tpu_custom_call" | custom-call | tf_op jit(solution)/shard_map/pallas_call | solution.py:302

commit v2 on v1

v2 whole, which is shorter than its diff:
```python
import functools
import math

import jax
import jax.numpy as jnp
from jax import lax
from jax.experimental import pallas as pl
from jax.experimental.pallas import tpu as pltpu
from jax.sharding import PartitionSpec as P

MESH = pl.DeviceIdType.MESH
CHUNKS = 2
SLABS = 4
STEP_ROWS = 32


def chip_at(cycle, place, side):
    major = lax.div(place, side)
    minor = lax.rem(place - major + side, side)
    y, x = (minor, major) if cycle == 0 else (major, minor)
    return y * side + x


def place_of(cycle, chip, side):
    y, x = lax.div(chip, side), lax.rem(chip, side)
    major, minor = (x, y) if cycle == 0 else (y, x)
    return major * side + lax.rem(minor + major, side)


def gather_kernel(
    ranks, d_model,
    mix_hbm, gain_hbm, oq, tq, ok, tk, ov, tv,
    sq, sk, sv, cq, ck, cv,
    coefs, q_in, kv_in, col_a, col_b, sums,
    load_sem, stat_sem, ring_sem, twin_sem, ring_recv,
):
    me = lax.axis_index("rows")
    chips = ranks // 2
    side = math.isqrt(chips)
    steps = chips // 2
    chip, core = lax.div(me, 2), lax.rem(me, 2)
    twin = chip * 2 + 1 - core
    rows, q_cols = oq.shape
    kv_cols = ok.shape[0]
    half = rows // 2
    chunk = half // CHUNKS
    slab = rows // SLABS
    tiles = q_cols // 128
    one, one_kv = q_in.at[0], kv_in.at[0]

    barrier = pltpu.get_barrier_semaphore()
    for shift in range(1, ranks):
        pl.semaphore_signal(
            barrier, inc=1, device_id={"rows": lax.rem(me + shift, ranks)}, device_id_type=MESH
        )

    def load(source, held, sem):
        pltpu.make_async_copy(source, held, sem).start()

    def settle(ref, sem):
        pltpu.make_async_copy(ref, ref, sem).wait()

    load(mix_hbm, coefs.at[0], load_sem.at[0])
    load(gain_hbm, coefs.at[1], load_sem.at[0])
    for s in range(SLABS):
        r = pl.ds(s * slab, slab)
        for n, source in enumerate((oq, tq)):
            load(source.at[r], q_in.at[n, r], load_sem.at[2 + s])
    for n, source in enumerate((ok, tk, ov, tv)):
        load(source, kv_in.at[n % 2, pl.ds(n // 2 * kv_cols, kv_cols)], load_sem.at[1])

    settle(coefs, load_sem.at[0])
    a_row = coefs[1] * coefs[0]
    b_row = coefs[1] * (1.0 - coefs[0])
    for c in range(0, rows, 128):
        col_a[pl.ds(c, 128), :] = jnp.broadcast_to(a_row[:, c:c + 128], (128, 128)).T
        col_b[pl.ds(c, 128), :] = jnp.broadcast_to(b_row[:, c:c + 128], (128, 128)).T

    accs = tuple(jnp.zeros((8, 128), jnp.float32) for _ in range(tiles))
    for s in range(SLABS):
        settle(q_in.at[:, pl.ds(s * slab, slab)], load_sem.at[2 + s])

        def body(i, accs):
            r = pl.ds(pl.multiple_of(s * slab + i * STEP_ROWS, STEP_ROWS), STEP_ROWS)
            a, b = col_a[r, :], col_b[r, :]
            new = []
            for j, acc in enumerate(accs):
                c = pl.ds(j * 128, 128)
                f = a * q_in[0, r, c] + b * q_in[1, r, c]
                one[r, c] = f
                new.append(acc + jnp.sum(jnp.abs(f).reshape(STEP_ROWS // 8, 8, 128), axis=0))
            return tuple(new)

        accs = lax.fori_loop(0, slab // STEP_ROWS, body, accs)
    for j, acc in enumerate(accs):
        sums[me, pl.ds(j, 1), :] = jnp.sum(acc, axis=0, keepdims=True)
    settle(kv_in, load_sem.at[1])
    f = a_row * kv_in[0] + b_row * kv_in[1]
    one_kv[...] = f
    sizes = jnp.abs(f)
    size = sizes[:, 0:128]
    for c in range(128, rows, 128):
        size = size + sizes[:, c:c + 128]
    sums[me, pl.ds(tiles, 1), :] = jnp.sum(size.T, axis=0, keepdims=True)

    def remote(src, dst, send, recv, device):
        pltpu.make_async_remote_copy(
            src_ref=src, dst_ref=dst, send_sem=send, recv_sem=recv,
            device_id={"rows": device}, device_id_type=MESH,
        ).start()

    pl.semaphore_wait(barrier, ranks - 1)
    place = sums.at[me, pl.ds(0, tiles + 1)]
    for shift in range(1, ranks):
        remote(place, place, stat_sem.at[0], stat_sem.at[1], lax.rem(me + shift, ranks))

    spots = [place_of(c, chip, side) for c in range(2)]
    aims = {}
    for c in range(2):
        aims[c, 0] = chip_at(c, lax.rem(spots[c] + 1, chips), side) * 2 + core
        aims[c, 1] = chip_at(c, lax.rem(spots[c] + chips - 1, chips), side) * 2 + core

    peers = sums.at[pl.ds(0, ranks - 1), pl.ds(0, tiles + 1)]
    settle(peers, stat_sem.at[1])
    total = sums[0, 0:tiles + 1, :]
    for owner in range(1, ranks):
        total = total + sums[owner, 0:tiles + 1, :]
    scale = total / d_model
    inverse = 1.0 / scale

    def pieces(step, way):
        if step < steps:
            order = range(CHUNKS) if way == 0 else range(CHUNKS - 1, -1, -1)
            return [(n * chunk, chunk, 2 if at == 0 else None) for at, n in enumerate(order)]
        part = half // 4
        firsts = (0, part) if way == 0 else (half - part, half - 2 * part)
        return [(first, part, way if at == 0 else None) for at, first in enumerate(firsts)]

    def refs(c, dev, item):
        first, count, share = item
        at = pl.multiple_of(dev * rows + c * half + first, 32)
        out = [sq.at[pl.ds(at, count)]]
        if share is not None:
            at = pl.ds(pl.multiple_of(dev * rows, rows), rows)
            ref = (sk, sv)[c]
            if share < 2:
                ref = ref.at[pl.ds(share * (kv_cols // 2), kv_cols // 2)]
            out.append(ref.at[:, at])
        return out

    def ring(c, way, step, at, dev):
        for ref in refs(c, dev, pieces(step, way)[at]):
            remote(ref, ref, ring_sem.at[0], ring_recv.at[c, way, step - 1, at], aims[c, way])

    def settle_ring(c, way, step, at):
        first, count, share = pieces(step, way)[at]
        extra = 0 if share is None else kv_cols * rows // q_cols // (1 if share == 2 else 2)
        settle(sq.at[pl.ds(0, count + extra)], ring_recv.at[c, way, step - 1, at])

    def pass_on(c, dev, item):
        for ref in refs(c, dev, item):
            remote(ref, ref, twin_sem.at[0], twin_sem.at[1], twin)

    flip = jnp.broadcast_to(inverse[tiles:tiles + 1, :], (128, 128)).T
    own = pl.multiple_of(me * rows, rows)
    for c, ref in enumerate((sk, sv)):
        r = pl.ds(c * kv_cols, kv_cols)
        for col in range(0, rows, 128):
            ref[:, pl.ds(pl.multiple_of(own + col, 128), 128)] = (
                one_kv[r, pl.ds(col, 128)] * flip[c * kv_cols:(c + 1) * kv_cols, :]
            ).astype(jnp.bfloat16)
    made = set()
    sent = set()
    for n in [k for pair in zip(range(CHUNKS), range(CHUNKS - 1, -1, -1)) for k in pair]:
        if n in made:
            continue
        made.add(n)
        for c in range(2):
            def body(i, carry, c=c, n=n):
                first = c * half + n * chunk + i * STEP_ROWS
                r = pl.ds(pl.multiple_of(first, STEP_ROWS), STEP_ROWS)
                to = pl.ds(pl.multiple_of(me * rows + first, STEP_ROWS), STEP_ROWS)
                for j in range(tiles):
                    col = pl.ds(j * 128, 128)
                    sq[to, col] = (one[r, col] * inverse[j:j + 1, :]).astype(jnp.bfloat16)
                return carry

            lax.fori_loop(0, chunk // STEP_ROWS, body, 0)
        for at in range(CHUNKS):
            for c in range(2):
                for way in range(2):
                    ready = {(k[0] // chunk) for k in pieces(1, way)[:at + 1]}
                    if ready <= made and (c, way, at) not in sent:
                        sent.add((c, way, at))
                        ring(c, way, 1, at, me)
    for c in range(2):
        pass_on(c, me, (0, half, 2))

    for j in range(tiles):
        cq[:, pl.ds(j * 128, 128)] = scale[j:j + 1, :]
    ck[...] = scale[tiles:tiles + 1, 0:kv_cols]
    cv[...] = scale[tiles:tiles + 1, kv_cols:2 * kv_cols]

    for step in range(1, steps + 1):
        devs = {}
        for c in range(2):
            devs[c, 0] = chip_at(c, lax.rem(spots[c] + chips - step, chips), side) * 2 + core
            devs[c, 1] = chip_at(c, lax.rem(spots[c] + step, chips), side) * 2 + core
        for at in range(len(pieces(step, 0))):
            for c in range(2):
                for way in range(2):
                    settle_ring(c, way, step, at)
                    item = pieces(step, way)[at]
                    if step < steps:
                        for later, nxt in enumerate(pieces(step + 1, way)):
                            if item[0] <= nxt[0] < item[0] + item[1]:
                                ring(c, way, step + 1, later, devs[c, way])
                    pass_on(c, devs[c, way], item)
    settle(peers, stat_sem.at[0])
    share = half + kv_cols * rows // q_cols
    settle(sq.at[pl.ds(0, 2 * (chips - 1) * share)], ring_sem.at[0])
    settle(sq.at[pl.ds(0, 2 * chips * share)], twin_sem.at[0])
    settle(sq.at[pl.ds(0, 2 * chips * share)], twin_sem.at[1])


def write_kernel(sq, sk, sv, cq, ck, cv, oq, ok, ov, dq, dk, dv, q_sem, sem):
    count = q_sem.shape[0]
    rows = sq.shape[0] // count
    copies = []
    for n in range(count):
        r = pl.ds(n * rows, rows)
        copies.append(pltpu.make_async_copy(sq.at[r], oq.at[r], q_sem.at[n]))
    for n, (source, out) in enumerate(((sk, ok), (sv, ov), (cq, dq), (ck, dk), (cv, dv))):
        copies.append(pltpu.make_async_copy(source, out, sem.at[n]))
    for copy in copies:
        copy.start()
    for copy in copies:
        copy.wait()


def local(ranks, d_model, one_query, other_query, one_key, other_key, one_value, other_value, mix_share, norm_gain):
    rows, q_cols = one_query.shape
    kv_cols = one_key.shape[1]
    whole = ranks * rows
    steps = ranks // 4
    vmem = pl.BlockSpec(memory_space=pltpu.VMEM)
    hbm = pl.BlockSpec(memory_space=pltpu.HBM)
    dma = pltpu.SemaphoreType.DMA
    f32, bf16 = jnp.float32, jnp.bfloat16
    shapes = (
        jax.ShapeDtypeStruct((whole, q_cols), bf16),
        jax.ShapeDtypeStruct((kv_cols, whole), bf16),
        jax.ShapeDtypeStruct((kv_cols, whole), bf16),
        jax.ShapeDtypeStruct((1, q_cols), f32),
        jax.ShapeDtypeStruct((1, kv_cols), f32),
        jax.ShapeDtypeStruct((1, kv_cols), f32),
    )
    landed = pl.pallas_call(
        functools.partial(gather_kernel, ranks, d_model),
        out_shape=tuple(pltpu.VMEM(x.shape, x.dtype) for x in shapes),
        in_specs=[hbm] * 8,
        out_specs=(vmem,) * 6,
        scratch_shapes=[
            pltpu.VMEM((2, 1, rows), f32),
            pltpu.VMEM((2, rows, q_cols), f32),
            pltpu.VMEM((2, 2 * kv_cols, rows), f32),
            pltpu.VMEM((rows, 128), f32),
            pltpu.VMEM((rows, 128), f32),
            pltpu.VMEM((ranks, 16, 128), f32),
            dma((2 + SLABS,)),
            dma((2,)),
            dma((1,)),
            dma((2,)),
            dma((2, 2, steps, max(CHUNKS, 2))),
        ],
        compiler_params=pltpu.CompilerParams(
            collective_id=0, has_side_effects=True, vmem_limit_bytes=VMEM_A
        ),
    )(*(
        pltpu.with_memory_space_constraint(x, pltpu.HBM)
        for x in (
            mix_share.reshape(1, rows), norm_gain.reshape(1, rows), one_query, other_query,
            one_key.T, other_key.T, one_value.T, other_value.T,
        )
    ))
    out = pl.pallas_call(
        write_kernel,
        out_shape=shapes,
        in_specs=[vmem] * 6,
        out_specs=(hbm,) * 6,
        scratch_shapes=[dma((8,)), dma((5,))],
        compiler_params=pltpu.CompilerParams(vmem_limit_bytes=VMEM_B),
    )(*landed)
    sq, sk, sv, cq, ck, cv = out
    return sq, sk.T, sv.T, cq[0], ck[0], cv[0]


VMEM_A = 10 * 1024 * 1024
VMEM_B = 2 * 1024 * 1024


def solution(mesh):
    def body(one_query, *rest):
        ranks = mesh.shape["rows"]
        return local(ranks, ranks * one_query.shape[0], one_query, *rest)

    return jax.shard_map(
        body,
        mesh=mesh,
        in_specs=(P("rows", "cols"),) * 6 + (P("rows"),) * 2,
        out_specs=(P(None, "cols"),) * 3 + (P("cols"),) * 3,
        check_vma=False,
    )
```

time: 77.1 us -> 71.7 us (0.930)
  Pallas kernels: 76.3 us -> 70.9 us
    pallas_call x1, Pallas kernels: 69.7 us -> 64.3 us  [local(): pl.pallas_call(functools.partial(gather_kernel, ranks, d_model), out_shap...]
where the time goes in v2:
time: 71.7 us; the launch traced here: 71.6 us
  Pallas kernels  70.9 us (99%)
    pallas_call x1, Pallas kernels, local(): pl.pallas_call(functools.partial(gather_kernel, ranks, d_model), out_shap...  64.3 us
    pallas_call x1, Pallas kernels, local(): pl.pallas_call(write_kernel, out_shape=shapes, in_specs=[vmem] * 6, out_s...  6.62 us

profile of v2, /device:TPU:1, one launch (start us, length us, event | category | flops | bytes accessed | tf_op | source)
XLA Modules:
  0.0 71.6 jit_solution(7229542884953792987)
XLA Ops:
  0.6 64.3 %shard_map.127 = (bf16[8192,1024]{1,0:T(8,128)(2,1)S(1)}, bf16[64,8192]{1,0:T(8,128)(2,1)S(1)}, bf16[64,8192]{1,0:T(8,128)(2,1)S(1)}, f32[1,1024]{1,0:T(1,128)S(...) custom-call(f32[1,256]{1,0:T(1,128)} %bitcast.15, f32[1,256]{1,0:T(1,128)} %bitcast.16, f32[256,1024]{1,0:T(8,128)} %oq.1, ...), custom_call_target="tpu_custom_call" | custom-call | tf_op jit(solution)/shard_map/pallas_call | solution.py:258
  65.0 6.6 %shard_map.128 = (bf16[8192,1024]{1,0:T(8,128)(2,1)}, bf16[64,8192]{1,0:T(8,128)(2,1)}, bf16[64,8192]{1,0:T(8,128)(2,1)}, f32[1,1024]{1,0:T(1,128)}, f32[1,64]{1,0:T(1,128)}, /*index=5*/f32[1,64]{1,0:T(1,128)}) custom-call(bf16[8192,1024]{1,0:T(8,128)(2,1)S(1)} %get-tuple-element.18.sq, bf16[64,8192]{1,0:T(8,128)(2,1)S(1)} %get-tuple-element.19.sk, ...), custom_call_target="tpu_custom_call" | custom-call | tf_op jit(solution)/shard_map/pallas_call | solution.py:286

commit v3 on v2

--- a/solution.py
+++ b/solution.py
@@ -9,7 +9,7 @@
 from jax.sharding import PartitionSpec as P
 
 MESH = pl.DeviceIdType.MESH
-CHUNKS = 2
+EARLY = 48
 SLABS = 4
 STEP_ROWS = 32
 
@@ -32,7 +32,8 @@
     mix_hbm, gain_hbm, oq, tq, ok, tk, ov, tv,
     sq, sk, sv, cq, ck, cv,
     coefs, q_in, kv_in, col_a, col_b, sums,
-    load_sem, stat_sem, ring_sem, twin_sem, ring_recv,
+    early,
+    load_sem, stat_sem, ring_sem, twin_sem, ring_recv, early_sem,
 ):
     me = lax.axis_index("rows")
     chips = ranks // 2
@@ -43,7 +44,6 @@
     rows, q_cols = oq.shape
     kv_cols = ok.shape[0]
     half = rows // 2
-    chunk = half // CHUNKS
     slab = rows // SLABS
     tiles = q_cols // 128
     one, one_kv = q_in.at[0], kv_in.at[0]
@@ -120,6 +120,14 @@
         aims[c, 0] = chip_at(c, lax.rem(spots[c] + 1, chips), side) * 2 + core
         aims[c, 1] = chip_at(c, lax.rem(spots[c] + chips - 1, chips), side) * 2 + core
 
+    def early_rows(way):
+        return 0 if way == 0 else half - EARLY
+
+    for c in range(2):
+        for way in range(2):
+            remote(one.at[pl.ds(c * half + early_rows(way), EARLY)], early.at[c, way],
+                   ring_sem.at[1], early_sem.at[c, way], aims[c, way])
+
     peers = sums.at[pl.ds(0, ranks - 1), pl.ds(0, tiles + 1)]
     settle(peers, stat_sem.at[1])
     total = sums[0, 0:tiles + 1, :]
@@ -130,16 +138,21 @@
 
     def pieces(step, way):
         if step < steps:
-            order = range(CHUNKS) if way == 0 else range(CHUNKS - 1, -1, -1)
-            return [(n * chunk, chunk, 2 if at == 0 else None) for at, n in enumerate(order)]
-        part = half // 4
-        firsts = (0, part) if way == 0 else (half - part, half - 2 * part)
-        return [(first, part, way if at == 0 else None) for at, first in enumerate(firsts)]
+            cut = half // 2
+            cuts = [(0, cut, 2), (cut, half - cut, None)]
+            if step == 1:
+                cuts[0] = (EARLY, cut - EARLY, 2)
+        else:
+            cut = half // 4
+            cuts = [(0, cut, way), (cut, half // 2 - cut, None)]
+        if way == 0:
+            return cuts
+        return [(half - first - count, count, share) for first, count, share in cuts]
 
     def refs(c, dev, item):
         first, count, share = item
-        at = pl.multiple_of(dev * rows + c * half + first, 32)
-        out = [sq.at[pl.ds(at, count)]]
+        at = pl.multiple_of(dev * rows + c * half + first, 16)
+        out = [sq.at[pl.ds(at, count)]] if count else []
         if share is not None:
             at = pl.ds(pl.multiple_of(dev * rows, rows), rows)
             ref = (sk, sv)[c]
@@ -161,38 +174,36 @@
         for ref in refs(c, dev, item):
             remote(ref, ref, twin_sem.at[0], twin_sem.at[1], twin)
 
+    def narrow(source, first, dev, to, count):
+        def body(i, carry):
+            r = pl.ds(pl.multiple_of(first + i * 16, 16), 16)
+            out = pl.ds(pl.multiple_of(dev * rows + to + i * 16, 16), 16)
+            for j in range(tiles):
+                col = pl.ds(j * 128, 128)
+                sq[out, col] = (source[r, col] * inverse[j:j + 1, :]).astype(jnp.bfloat16)
+            return carry
+
+        lax.fori_loop(0, count // 16, body, 0)
+
     flip = jnp.broadcast_to(inverse[tiles:tiles + 1, :], (128, 128)).T
-    own = pl.multiple_of(me * rows, rows)
-    for c, ref in enumerate((sk, sv)):
-        r = pl.ds(c * kv_cols, kv_cols)
+
+    def narrow_kv(c, source, dev):
+        at = pl.multiple_of(dev * rows, rows)
         for col in range(0, rows, 128):
-            ref[:, pl.ds(pl.multiple_of(own + col, 128), 128)] = (
-                one_kv[r, pl.ds(col, 128)] * flip[c * kv_cols:(c + 1) * kv_cols, :]
+            (sk, sv)[c][:, pl.ds(pl.multiple_of(at + col, 128), 128)] = (
+                source[:, pl.ds(col, 128)] * flip[c * kv_cols:(c + 1) * kv_cols, :]
             ).astype(jnp.bfloat16)
-    made = set()
-    sent = set()
-    for n in [k for pair in zip(range(CHUNKS), range(CHUNKS - 1, -1, -1)) for k in pair]:
-        if n in made:
-            continue
-        made.add(n)
-        for c in range(2):
-            def body(i, carry, c=c, n=n):
-                first = c * half + n * chunk + i * STEP_ROWS
-                r = pl.ds(pl.multiple_of(first, STEP_ROWS), STEP_ROWS)
-                to = pl.ds(pl.multiple_of(me * rows + first, STEP_ROWS), STEP_ROWS)
-                for j in range(tiles):
-                    col = pl.ds(j * 128, 128)
-                    sq[to, col] = (one[r, col] * inverse[j:j + 1, :]).astype(jnp.bfloat16)
-                return carry
-
-            lax.fori_loop(0, chunk // STEP_ROWS, body, 0)
-        for at in range(CHUNKS):
-            for c in range(2):
-                for way in range(2):
-                    ready = {(k[0] // chunk) for k in pieces(1, way)[:at + 1]}
-                    if ready <= made and (c, way, at) not in sent:
-                        sent.add((c, way, at))
-                        ring(c, way, 1, at, me)
+
+    def origins(c, step):
+        back = chip_at(c, lax.rem(spots[c] + chips - step, chips), side) * 2 + core
+        return back, chip_at(c, lax.rem(spots[c] + step, chips), side) * 2 + core
+
+    for c in range(2):
+        narrow_kv(c, one_kv.at[pl.ds(c * kv_cols, kv_cols)], me)
+        narrow(one, c * half, me, c * half, half)
+        for at in range(2):
+            for way in range(2):
+                ring(c, way, 1, at, me)
     for c in range(2):
         pass_on(c, me, (0, half, 2))
 
@@ -202,23 +213,27 @@
     cv[...] = scale[tiles:tiles + 1, kv_cols:2 * kv_cols]
 
     for step in range(1, steps + 1):
-        devs = {}
-        for c in range(2):
-            devs[c, 0] = chip_at(c, lax.rem(spots[c] + chips - step, chips), side) * 2 + core
-            devs[c, 1] = chip_at(c, lax.rem(spots[c] + step, chips), side) * 2 + core
-        for at in range(len(pieces(step, 0))):
+        devs = {c: origins(c, step) for c in range(2)}
+        for at in range(2):
             for c in range(2):
                 for way in range(2):
+                    dev = devs[c][way]
+                    if step == 1 and at == 0:
+                        settle(q_in.at[0, pl.ds(0, EARLY)], early_sem.at[c, way])
+                        narrow(early.at[c, way], 0, dev, c * half + early_rows(way), EARLY)
                     settle_ring(c, way, step, at)
                     item = pieces(step, way)[at]
+                    if step == 1:
+                        item = pieces(0, way)[at]
                     if step < steps:
                         for later, nxt in enumerate(pieces(step + 1, way)):
                             if item[0] <= nxt[0] < item[0] + item[1]:
-                                ring(c, way, step + 1, later, devs[c, way])
-                    pass_on(c, devs[c, way], item)
+                                ring(c, way, step + 1, later, dev)
+                    pass_on(c, dev, item)
     settle(peers, stat_sem.at[0])
     share = half + kv_cols * rows // q_cols
-    settle(sq.at[pl.ds(0, 2 * (chips - 1) * share)], ring_sem.at[0])
+    settle(sq.at[pl.ds(0, 2 * (chips - 1) * share - 4 * EARLY)], ring_sem.at[0])
+    settle(q_in.at[:, pl.ds(0, 2 * EARLY)], ring_sem.at[1])
     settle(sq.at[pl.ds(0, 2 * chips * share)], twin_sem.at[0])
     settle(sq.at[pl.ds(0, 2 * chips * share)], twin_sem.at[1])
 
@@ -267,11 +282,13 @@
             pltpu.VMEM((rows, 128), f32),
             pltpu.VMEM((rows, 128), f32),
             pltpu.VMEM((ranks, 16, 128), f32),
+            pltpu.VMEM((2, 2, EARLY, q_cols), f32),
             dma((2 + SLABS,)),
             dma((2,)),
-            dma((1,)),
             dma((2,)),
-            dma((2, 2, steps, max(CHUNKS, 2))),
+            dma((2,)),
+            dma((2, 2, steps, 2)),
+            dma((2, 2)),
         ],
         compiler_params=pltpu.CompilerParams(
             collective_id=0, has_side_effects=True, vmem_limit_bytes=VMEM_A

time: 71.7 us -> 70.2 us (0.979)
  Pallas kernels: 70.9 us -> 69.4 us
    pallas_call x1, Pallas kernels: 64.3 us -> 62.8 us  [local(): pl.pallas_call(functools.partial(gather_kernel, ranks, d_model), out_shap...]
where the time goes in v3:
time: 70.2 us; the launch traced here: 70.1 us
  Pallas kernels  69.4 us (99%)
    pallas_call x1, Pallas kernels, local(): pl.pallas_call(functools.partial(gather_kernel, ranks, d_model), out_shap...  62.8 us
    pallas_call x1, Pallas kernels, local(): pl.pallas_call(write_kernel, out_shape=shapes, in_specs=[vmem] * 6, out_s...  6.62 us

profile of v3, /device:TPU:1, one launch (start us, length us, event | category | flops | bytes accessed | tf_op | source)
XLA Modules:
  0.0 70.1 jit_solution(5023513891461019622)
XLA Ops:
  0.6 62.8 %shard_map.127 = (bf16[8192,1024]{1,0:T(8,128)(2,1)S(1)}, bf16[64,8192]{1,0:T(8,128)(2,1)S(1)}, bf16[64,8192]{1,0:T(8,128)(2,1)S(1)}, f32[1,1024]{1,0:T(1,128)S(...) custom-call(f32[1,256]{1,0:T(1,128)} %bitcast.15, f32[1,256]{1,0:T(1,128)} %bitcast.16, f32[256,1024]{1,0:T(8,128)} %oq.1, ...), custom_call_target="tpu_custom_call" | custom-call | tf_op jit(solution)/shard_map/pallas_call | solution.py:273
  63.5 6.6 %shard_map.128 = (bf16[8192,1024]{1,0:T(8,128)(2,1)}, bf16[64,8192]{1,0:T(8,128)(2,1)}, bf16[64,8192]{1,0:T(8,128)(2,1)}, f32[1,1024]{1,0:T(1,128)}, f32[1,64]{1,0:T(1,128)}, /*index=5*/f32[1,64]{1,0:T(1,128)}) custom-call(bf16[8192,1024]{1,0:T(8,128)(2,1)S(1)} %get-tuple-element.18.sq, bf16[64,8192]{1,0:T(8,128)(2,1)S(1)} %get-tuple-element.19.sk, ...), custom_call_target="tpu_custom_call" | custom-call | tf_op jit(solution)/shard_map/pallas_call | solution.py:303

commit v4 on v3

--- a/solution.py
+++ b/solution.py
@@ -10,7 +10,8 @@
 
 MESH = pl.DeviceIdType.MESH
 EARLY = 48
-SLABS = 4
+SLABS = 2
+WRITES = 32
 STEP_ROWS = 32
 
 
@@ -48,11 +49,20 @@
     tiles = q_cols // 128
     one, one_kv = q_in.at[0], kv_in.at[0]
 
+    y, x = lax.div(chip, side), lax.rem(chip, side)
+    hops = [min(k, side - k) for k in range(side)]
+    away = sorted(
+        ((dy, dx) for dy in range(side) for dx in range(side) if dy or dx),
+        key=lambda d: -(hops[d[0]] + hops[d[1]]),
+    )
+    others = [
+        (lax.rem(y + dy, side) * side + lax.rem(x + dx, side)) * 2 + k
+        for dy, dx in away for k in range(2)
+    ] + [twin]
+
     barrier = pltpu.get_barrier_semaphore()
-    for shift in range(1, ranks):
-        pl.semaphore_signal(
-            barrier, inc=1, device_id={"rows": lax.rem(me + shift, ranks)}, device_id_type=MESH
-        )
+    for dev in others:
+        pl.semaphore_signal(barrier, inc=1, device_id={"rows": dev}, device_id_type=MESH)
 
     def load(source, held, sem):
         pltpu.make_async_copy(source, held, sem).start()
@@ -111,8 +121,8 @@
 
     pl.semaphore_wait(barrier, ranks - 1)
     place = sums.at[me, pl.ds(0, tiles + 1)]
-    for shift in range(1, ranks):
-        remote(place, place, stat_sem.at[0], stat_sem.at[1], lax.rem(me + shift, ranks))
+    for dev in others:
+        remote(place, place, stat_sem.at[0], stat_sem.at[1], dev)
 
     spots = [place_of(c, chip, side) for c in range(2)]
     aims = {}
@@ -163,12 +173,12 @@
 
     def ring(c, way, step, at, dev):
         for ref in refs(c, dev, pieces(step, way)[at]):
-            remote(ref, ref, ring_sem.at[0], ring_recv.at[c, way, step - 1, at], aims[c, way])
-
-    def settle_ring(c, way, step, at):
+            remote(ref, ref, ring_sem.at[0], ring_recv.at[way, step - 1, at], aims[c, way])
+
+    def settle_ring(way, step, at):
         first, count, share = pieces(step, way)[at]
         extra = 0 if share is None else kv_cols * rows // q_cols // (1 if share == 2 else 2)
-        settle(sq.at[pl.ds(0, count + extra)], ring_recv.at[c, way, step - 1, at])
+        settle(sq.at[pl.ds(0, 2 * (count + extra))], ring_recv.at[way, step - 1, at])
 
     def pass_on(c, dev, item):
         for ref in refs(c, dev, item):
@@ -215,21 +225,20 @@
     for step in range(1, steps + 1):
         devs = {c: origins(c, step) for c in range(2)}
         for at in range(2):
-            for c in range(2):
-                for way in range(2):
-                    dev = devs[c][way]
-                    if step == 1 and at == 0:
+            for way in range(2):
+                if step == 1 and at == 0:
+                    for c in range(2):
                         settle(q_in.at[0, pl.ds(0, EARLY)], early_sem.at[c, way])
-                        narrow(early.at[c, way], 0, dev, c * half + early_rows(way), EARLY)
-                    settle_ring(c, way, step, at)
-                    item = pieces(step, way)[at]
-                    if step == 1:
-                        item = pieces(0, way)[at]
+                        narrow(early.at[c, way], 0, devs[c][way], c * half + early_rows(way), EARLY)
+                settle_ring(way, step, at)
+                item = pieces(min(step, steps) if step > 1 else 0, way)[at]
+                for c in range(2):
                     if step < steps:
                         for later, nxt in enumerate(pieces(step + 1, way)):
                             if item[0] <= nxt[0] < item[0] + item[1]:
-                                ring(c, way, step + 1, later, dev)
-                    pass_on(c, dev, item)
+                                ring(c, way, step + 1, later, devs[c][way])
+                for c in range(2):
+                    pass_on(c, devs[c][way], item)
     settle(peers, stat_sem.at[0])
     share = half + kv_cols * rows // q_cols
     settle(sq.at[pl.ds(0, 2 * (chips - 1) * share - 4 * EARLY)], ring_sem.at[0])
@@ -238,19 +247,16 @@
     settle(sq.at[pl.ds(0, 2 * chips * share)], twin_sem.at[1])
 
 
-def write_kernel(sq, sk, sv, cq, ck, cv, oq, ok, ov, dq, dk, dv, q_sem, sem):
-    count = q_sem.shape[0]
-    rows = sq.shape[0] // count
-    copies = []
-    for n in range(count):
+def write_kernel(sq, sk, sv, cq, ck, cv, oq, ok, ov, dq, dk, dv, sem):
+    rows = sq.shape[0] // WRITES
+    pairs = [(cq, dq), (ck, dk), (cv, dv), (sk, ok), (sv, ov)]
+    for n in range(WRITES):
         r = pl.ds(n * rows, rows)
-        copies.append(pltpu.make_async_copy(sq.at[r], oq.at[r], q_sem.at[n]))
-    for n, (source, out) in enumerate(((sk, ok), (sv, ov), (cq, dq), (ck, dk), (cv, dv))):
-        copies.append(pltpu.make_async_copy(source, out, sem.at[n]))
-    for copy in copies:
-        copy.start()
-    for copy in copies:
-        copy.wait()
+        pairs.append((sq.at[r], oq.at[r]))
+    for n, (source, out) in enumerate(pairs):
+        pltpu.make_async_copy(source, out, sem.at[min(n, 5)]).start()
+    for n, (source, out) in enumerate(pairs[:5] + [(sq, oq)]):
+        pltpu.make_async_copy(source, out, sem.at[n]).wait()
 
 
 def local(ranks, d_model, one_query, other_query, one_key, other_key, one_value, other_value, mix_share, norm_gain):
@@ -287,7 +293,7 @@
             dma((2,)),
             dma((2,)),
             dma((2,)),
-            dma((2, 2, steps, 2)),
+            dma((2, steps, 2)),
             dma((2, 2)),
         ],
         compiler_params=pltpu.CompilerParams(
@@ -305,7 +311,7 @@
         out_shape=shapes,
         in_specs=[vmem] * 6,
         out_specs=(hbm,) * 6,
-        scratch_shapes=[dma((8,)), dma((5,))],
+        scratch_shapes=[dma((6,))],
         compiler_params=pltpu.CompilerParams(vmem_limit_bytes=VMEM_B),
     )(*landed)
     sq, sk, sv, cq, ck, cv = out

time: 70.2 us -> 69.2 us (0.986)
  Pallas kernels: 69.4 us -> 68.5 us
    pallas_call x1, Pallas kernels: 62.8 us -> 62 us  [local(): pl.pallas_call(functools.partial(gather_kernel, ranks, d_model), out_shap...]
where the time goes in v4:
time: 69.2 us; the launch traced here: 69.1 us
  Pallas kernels  68.5 us (99%)
    pallas_call x1, Pallas kernels, local(): pl.pallas_call(functools.partial(gather_kernel, ranks, d_model), out_shap...  62 us
    pallas_call x1, Pallas kernels, local(): pl.pallas_call(write_kernel, out_shape=shapes, in_specs=[vmem] * 6, out_s...  6.49 us

profile of v4, /device:TPU:1, one launch (start us, length us, event | category | flops | bytes accessed | tf_op | source)
XLA Modules:
  0.0 69.1 jit_solution(6663775370058227818)
XLA Ops:
  0.6 62.0 %shard_map.127 = (bf16[8192,1024]{1,0:T(8,128)(2,1)S(1)}, bf16[64,8192]{1,0:T(8,128)(2,1)S(1)}, bf16[64,8192]{1,0:T(8,128)(2,1)S(1)}, f32[1,1024]{1,0:T(1,128)S(...) custom-call(f32[1,256]{1,0:T(1,128)} %bitcast.15, f32[1,256]{1,0:T(1,128)} %bitcast.16, f32[256,1024]{1,0:T(8,128)} %oq.1, ...), custom_call_target="tpu_custom_call" | custom-call | tf_op jit(solution)/shard_map/pallas_call | solution.py:279
  62.6 6.5 %shard_map.128 = (bf16[8192,1024]{1,0:T(8,128)(2,1)}, bf16[64,8192]{1,0:T(8,128)(2,1)}, bf16[64,8192]{1,0:T(8,128)(2,1)}, f32[1,1024]{1,0:T(1,128)}, f32[1,64]{1,0:T(1,128)}, /*index=5*/f32[1,64]{1,0:T(1,128)}) custom-call(bf16[8192,1024]{1,0:T(8,128)(2,1)S(1)} %get-tuple-element.18.sq, bf16[64,8192]{1,0:T(8,128)(2,1)S(1)} %get-tuple-element.19.sk, ...), custom_call_target="tpu_custom_call" | custom-call | tf_op jit(solution)/shard_map/pallas_call | solution.py:309

commit v5 on v4

--- a/solution.py
+++ b/solution.py
@@ -9,7 +9,7 @@
 from jax.sharding import PartitionSpec as P
 
 MESH = pl.DeviceIdType.MESH
-EARLY = 48
+EARLY = (48, 16)
 SLABS = 2
 WRITES = 32
 STEP_ROWS = 32
@@ -32,8 +32,7 @@
     ranks, d_model,
     mix_hbm, gain_hbm, oq, tq, ok, tk, ov, tv,
     sq, sk, sv, cq, ck, cv,
-    coefs, q_in, kv_in, col_a, col_b, sums,
-    early,
+    coefs, q_in, kv_in, col_a, col_b, line, column, early,
     load_sem, stat_sem, ring_sem, twin_sem, ring_recv, early_sem,
 ):
     me = lax.axis_index("rows")
@@ -50,18 +49,14 @@
     one, one_kv = q_in.at[0], kv_in.at[0]
 
     y, x = lax.div(chip, side), lax.rem(chip, side)
-    hops = [min(k, side - k) for k in range(side)]
-    away = sorted(
-        ((dy, dx) for dy in range(side) for dx in range(side) if dy or dx),
-        key=lambda d: -(hops[d[0]] + hops[d[1]]),
-    )
-    others = [
-        (lax.rem(y + dy, side) * side + lax.rem(x + dx, side)) * 2 + k
-        for dy, dx in away for k in range(2)
+    order = sorted(range(1, side), key=lambda k: -min(k, side - k))
+    row_peers = [
+        (y * side + lax.rem(x + k, side)) * 2 + n for k in order for n in range(2)
     ] + [twin]
+    column_peers = [(lax.rem(y + k, side) * side + x) * 2 + core for k in order]
 
     barrier = pltpu.get_barrier_semaphore()
-    for dev in others:
+    for dev in row_peers + column_peers:
         pl.semaphore_signal(barrier, inc=1, device_id={"rows": dev}, device_id_type=MESH)
 
     def load(source, held, sem):
@@ -86,6 +81,7 @@
         col_a[pl.ds(c, 128), :] = jnp.broadcast_to(a_row[:, c:c + 128], (128, 128)).T
         col_b[pl.ds(c, 128), :] = jnp.broadcast_to(b_row[:, c:c + 128], (128, 128)).T
 
+    spot = x * 2 + core
     accs = tuple(jnp.zeros((8, 128), jnp.float32) for _ in range(tiles))
     for s in range(SLABS):
         settle(q_in.at[:, pl.ds(s * slab, slab)], load_sem.at[2 + s])
@@ -103,7 +99,7 @@
 
         accs = lax.fori_loop(0, slab // STEP_ROWS, body, accs)
     for j, acc in enumerate(accs):
-        sums[me, pl.ds(j, 1), :] = jnp.sum(acc, axis=0, keepdims=True)
+        line[spot, pl.ds(j, 1), :] = jnp.sum(acc, axis=0, keepdims=True)
     settle(kv_in, load_sem.at[1])
     f = a_row * kv_in[0] + b_row * kv_in[1]
     one_kv[...] = f
@@ -111,7 +107,7 @@
     size = sizes[:, 0:128]
     for c in range(128, rows, 128):
         size = size + sizes[:, c:c + 128]
-    sums[me, pl.ds(tiles, 1), :] = jnp.sum(size.T, axis=0, keepdims=True)
+    line[spot, pl.ds(tiles, 1), :] = jnp.sum(size.T, axis=0, keepdims=True)
 
     def remote(src, dst, send, recv, device):
         pltpu.make_async_remote_copy(
@@ -119,9 +115,10 @@
             device_id={"rows": device}, device_id_type=MESH,
         ).start()
 
-    pl.semaphore_wait(barrier, ranks - 1)
-    place = sums.at[me, pl.ds(0, tiles + 1)]
-    for dev in others:
+    pl.semaphore_wait(barrier, len(row_peers) + len(column_peers))
+    lines = pl.ds(0, tiles + 1)
+    place = line.at[spot, lines]
+    for dev in row_peers:
         remote(place, place, stat_sem.at[0], stat_sem.at[1], dev)
 
     spots = [place_of(c, chip, side) for c in range(2)]
@@ -130,19 +127,36 @@
         aims[c, 0] = chip_at(c, lax.rem(spots[c] + 1, chips), side) * 2 + core
         aims[c, 1] = chip_at(c, lax.rem(spots[c] + chips - 1, chips), side) * 2 + core
 
+    ahead = sum(EARLY)
+
     def early_rows(way):
-        return 0 if way == 0 else half - EARLY
-
-    for c in range(2):
-        for way in range(2):
-            remote(one.at[pl.ds(c * half + early_rows(way), EARLY)], early.at[c, way],
-                   ring_sem.at[1], early_sem.at[c, way], aims[c, way])
-
-    peers = sums.at[pl.ds(0, ranks - 1), pl.ds(0, tiles + 1)]
-    settle(peers, stat_sem.at[1])
-    total = sums[0, 0:tiles + 1, :]
-    for owner in range(1, ranks):
-        total = total + sums[owner, 0:tiles + 1, :]
+        return 0 if way == 0 else half - ahead
+
+    def send_early(batch):
+        skip = sum(EARLY[:batch])
+        count = EARLY[batch]
+        for c in range(2):
+            for way in range(2):
+                at = skip if way == 0 else ahead - skip - count
+                remote(one.at[pl.ds(c * half + early_rows(way) + at, count)],
+                       early.at[c, way, pl.ds(at, count)],
+                       ring_sem.at[1], early_sem.at[batch, way], aims[c, way])
+
+    def gathered(ref, peers, sems):
+        slots = ref.at[pl.ds(0, peers), lines]
+        settle(slots, sems)
+        total = ref[0, 0:tiles + 1, :]
+        for n in range(1, peers + 1):
+            total = total + ref[n, 0:tiles + 1, :]
+        return total
+
+    send_early(0)
+    column[y, lines, :] = gathered(line, len(row_peers), stat_sem.at[1])
+    place = column.at[y, lines]
+    for dev in column_peers:
+        remote(place, place, stat_sem.at[2], stat_sem.at[3], dev)
+    send_early(1)
+    total = gathered(column, len(column_peers), stat_sem.at[3])
     scale = total / d_model
     inverse = 1.0 / scale
 
@@ -151,7 +165,7 @@
             cut = half // 2
             cuts = [(0, cut, 2), (cut, half - cut, None)]
             if step == 1:
-                cuts[0] = (EARLY, cut - EARLY, 2)
+                cuts[0] = (ahead, cut - ahead, 2)
         else:
             cut = half // 4
             cuts = [(0, cut, way), (cut, half // 2 - cut, None)]
@@ -227,9 +241,10 @@
         for at in range(2):
             for way in range(2):
                 if step == 1 and at == 0:
+                    for batch, count in enumerate(EARLY):
+                        settle(q_in.at[:, pl.ds(0, count)], early_sem.at[batch, way])
                     for c in range(2):
-                        settle(q_in.at[0, pl.ds(0, EARLY)], early_sem.at[c, way])
-                        narrow(early.at[c, way], 0, devs[c][way], c * half + early_rows(way), EARLY)
+                        narrow(early.at[c, way], 0, devs[c][way], c * half + early_rows(way), ahead)
                 settle_ring(way, step, at)
                 item = pieces(min(step, steps) if step > 1 else 0, way)[at]
                 for c in range(2):
@@ -239,10 +254,11 @@
                                 ring(c, way, step + 1, later, devs[c][way])
                 for c in range(2):
                     pass_on(c, devs[c][way], item)
-    settle(peers, stat_sem.at[0])
+    settle(line.at[pl.ds(0, len(row_peers)), lines], stat_sem.at[0])
+    settle(column.at[pl.ds(0, len(column_peers)), lines], stat_sem.at[2])
     share = half + kv_cols * rows // q_cols
-    settle(sq.at[pl.ds(0, 2 * (chips - 1) * share - 4 * EARLY)], ring_sem.at[0])
-    settle(q_in.at[:, pl.ds(0, 2 * EARLY)], ring_sem.at[1])
+    settle(sq.at[pl.ds(0, 2 * (chips - 1) * share - 4 * ahead)], ring_sem.at[0])
+    settle(q_in.at[:, pl.ds(0, 2 * ahead)], ring_sem.at[1])
     settle(sq.at[pl.ds(0, 2 * chips * share)], twin_sem.at[0])
     settle(sq.at[pl.ds(0, 2 * chips * share)], twin_sem.at[1])
 
@@ -264,6 +280,7 @@
     kv_cols = one_key.shape[1]
     whole = ranks * rows
     steps = ranks // 4
+    side = math.isqrt(ranks // 2)
     vmem = pl.BlockSpec(memory_space=pltpu.VMEM)
     hbm = pl.BlockSpec(memory_space=pltpu.HBM)
     dma = pltpu.SemaphoreType.DMA
@@ -287,10 +304,11 @@
             pltpu.VMEM((2, 2 * kv_cols, rows), f32),
             pltpu.VMEM((rows, 128), f32),
             pltpu.VMEM((rows, 128), f32),
-            pltpu.VMEM((ranks, 16, 128), f32),
-            pltpu.VMEM((2, 2, EARLY, q_cols), f32),
+            pltpu.VMEM((2 * side, 16, 128), f32),
+            pltpu.VMEM((side, 16, 128), f32),
+            pltpu.VMEM((2, 2, sum(EARLY), q_cols), f32),
             dma((2 + SLABS,)),
-            dma((2,)),
+            dma((4,)),
             dma((2,)),
             dma((2,)),
             dma((2, steps, 2)),

time: 69.2 us -> 68.4 us (0.988)
  Pallas kernels: 68.5 us -> 67.6 us
    pallas_call x1, Pallas kernels: 62 us -> 61.2 us  [local(): pl.pallas_call(functools.partial(gather_kernel, ranks, d_model), out_shap...]
where the time goes in v5:
time: 68.4 us; the launch traced here: 68.3 us
  Pallas kernels  67.6 us (99%)
    pallas_call x1, Pallas kernels, local(): pl.pallas_call(functools.partial(gather_kernel, ranks, d_model), out_shap...  61.2 us
    pallas_call x1, Pallas kernels, local(): pl.pallas_call(write_kernel, out_shape=shapes, in_specs=[vmem] * 6, out_s...  6.49 us

profile of v5, /device:TPU:1, one launch (start us, length us, event | category | flops | bytes accessed | tf_op | source)
XLA Modules:
  0.0 68.3 jit_solution(16438461489459929535)
XLA Ops:
  0.6 61.2 %shard_map.127 = (bf16[8192,1024]{1,0:T(8,128)(2,1)S(1)}, bf16[64,8192]{1,0:T(8,128)(2,1)S(1)}, bf16[64,8192]{1,0:T(8,128)(2,1)S(1)}, f32[1,1024]{1,0:T(1,128)S(...) custom-call(f32[1,256]{1,0:T(1,128)} %bitcast.15, f32[1,256]{1,0:T(1,128)} %bitcast.16, f32[256,1024]{1,0:T(8,128)} %oq.1, ...), custom_call_target="tpu_custom_call" | custom-call | tf_op jit(solution)/shard_map/pallas_call | solution.py:296
  61.8 6.5 %shard_map.128 = (bf16[8192,1024]{1,0:T(8,128)(2,1)}, bf16[64,8192]{1,0:T(8,128)(2,1)}, bf16[64,8192]{1,0:T(8,128)(2,1)}, f32[1,1024]{1,0:T(1,128)}, f32[1,64]{1,0:T(1,128)}, /*index=5*/f32[1,64]{1,0:T(1,128)}) custom-call(bf16[8192,1024]{1,0:T(8,128)(2,1)S(1)} %get-tuple-element.18.sq, bf16[64,8192]{1,0:T(8,128)(2,1)S(1)} %get-tuple-element.19.sk, ...), custom_call_target="tpu_custom_call" | custom-call | tf_op jit(solution)/shard_map/pallas_call | solution.py:327

commit v6 on v5

--- a/solution.py
+++ b/solution.py
@@ -9,8 +9,9 @@
 from jax.sharding import PartitionSpec as P
 
 MESH = pl.DeviceIdType.MESH
-EARLY = (48, 16)
-SLABS = 2
+EARLY = (32, 32)
+SLABS = 4
+PIECES = 4
 WRITES = 32
 STEP_ROWS = 32
 
@@ -67,12 +68,12 @@
 
     load(mix_hbm, coefs.at[0], load_sem.at[0])
     load(gain_hbm, coefs.at[1], load_sem.at[0])
+    for n, source in enumerate((ok, tk, ov, tv)):
+        load(source, kv_in.at[n % 2, pl.ds(n // 2 * kv_cols, kv_cols)], load_sem.at[1])
     for s in range(SLABS):
         r = pl.ds(s * slab, slab)
         for n, source in enumerate((oq, tq)):
             load(source.at[r], q_in.at[n, r], load_sem.at[2 + s])
-    for n, source in enumerate((ok, tk, ov, tv)):
-        load(source, kv_in.at[n % 2, pl.ds(n // 2 * kv_cols, kv_cols)], load_sem.at[1])
 
     settle(coefs, load_sem.at[0])
     a_row = coefs[1] * coefs[0]
@@ -82,6 +83,15 @@
         col_b[pl.ds(c, 128), :] = jnp.broadcast_to(b_row[:, c:c + 128], (128, 128)).T
 
     spot = x * 2 + core
+    settle(kv_in, load_sem.at[1])
+    f = a_row * kv_in[0] + b_row * kv_in[1]
+    one_kv[...] = f
+    sizes = jnp.abs(f)
+    size = sizes[:, 0:128]
+    for c in range(128, rows, 128):
+        size = size + sizes[:, c:c + 128]
+    line[spot, pl.ds(tiles, 1), :] = jnp.sum(size.T, axis=0, keepdims=True)
+
     accs = tuple(jnp.zeros((8, 128), jnp.float32) for _ in range(tiles))
     for s in range(SLABS):
         settle(q_in.at[:, pl.ds(s * slab, slab)], load_sem.at[2 + s])
@@ -100,14 +110,6 @@
         accs = lax.fori_loop(0, slab // STEP_ROWS, body, accs)
     for j, acc in enumerate(accs):
         line[spot, pl.ds(j, 1), :] = jnp.sum(acc, axis=0, keepdims=True)
-    settle(kv_in, load_sem.at[1])
-    f = a_row * kv_in[0] + b_row * kv_in[1]
-    one_kv[...] = f
-    sizes = jnp.abs(f)
-    size = sizes[:, 0:128]
-    for c in range(128, rows, 128):
-        size = size + sizes[:, c:c + 128]
-    line[spot, pl.ds(tiles, 1), :] = jnp.sum(size.T, axis=0, keepdims=True)
 
     def remote(src, dst, send, recv, device):
         pltpu.make_async_remote_copy(
@@ -161,14 +163,14 @@
     inverse = 1.0 / scale
 
     def pieces(step, way):
-        if step < steps:
-            cut = half // 2
-            cuts = [(0, cut, 2), (cut, half - cut, None)]
+        part = half // PIECES
+        cuts = []
+        for at in range(PIECES if step < steps else PIECES // 2):
+            first, last = at * part, (at + 1) * part
             if step == 1:
-                cuts[0] = (ahead, cut - ahead, 2)
-        else:
-            cut = half // 4
-            cuts = [(0, cut, way), (cut, half // 2 - cut, None)]
+                first = min(max(first, ahead), last)
+            share = None if at else (2 if step < steps else way)
+            cuts.append((first, last - first, share))
         if way == 0:
             return cuts
         return [(half - first - count, count, share) for first, count, share in cuts]
@@ -187,12 +189,14 @@
 
     def ring(c, way, step, at, dev):
         for ref in refs(c, dev, pieces(step, way)[at]):
-            remote(ref, ref, ring_sem.at[0], ring_recv.at[way, step - 1, at], aims[c, way])
-
-    def settle_ring(way, step, at):
-        first, count, share = pieces(step, way)[at]
-        extra = 0 if share is None else kv_cols * rows // q_cols // (1 if share == 2 else 2)
-        settle(sq.at[pl.ds(0, 2 * (count + extra))], ring_recv.at[way, step - 1, at])
+            remote(ref, ref, ring_sem.at[0], ring_recv.at[step - 1, at], aims[c, way])
+
+    def settle_ring(step, at):
+        first, count, share = pieces(step, 0)[at]
+        if share is not None:
+            count += kv_cols * rows // q_cols // (2 if step == steps else 1)
+        if count:
+            settle(sq.at[pl.ds(0, 4 * count)], ring_recv.at[step - 1, at])
 
     def pass_on(c, dev, item):
         for ref in refs(c, dev, item):
@@ -201,7 +205,7 @@
     def narrow(source, first, dev, to, count):
         def body(i, carry):
             r = pl.ds(pl.multiple_of(first + i * 16, 16), 16)
-            out = pl.ds(pl.multiple_of(dev * rows + to + i * 16, 16), 16)
+            out = pl.ds(pl.multiple_of(dev * rows + to + first + i * 16, 16), 16)
             for j in range(tiles):
                 col = pl.ds(j * 128, 128)
                 sq[out, col] = (source[r, col] * inverse[j:j + 1, :]).astype(jnp.bfloat16)
@@ -224,8 +228,8 @@
 
     for c in range(2):
         narrow_kv(c, one_kv.at[pl.ds(c * kv_cols, kv_cols)], me)
-        narrow(one, c * half, me, c * half, half)
-        for at in range(2):
+        narrow(one, c * half, me, 0, half)
+        for at in range(PIECES):
             for way in range(2):
                 ring(c, way, 1, at, me)
     for c in range(2):
@@ -238,20 +242,26 @@
 
     for step in range(1, steps + 1):
         devs = {c: origins(c, step) for c in range(2)}
-        for at in range(2):
+        for at in range(len(pieces(step, 0))):
+            if step == 1 and at < len(EARLY):
+                count = EARLY[at]
+                skip = sum(EARLY[:at])
+                for way in range(2):
+                    settle(q_in.at[:, pl.ds(0, count)], early_sem.at[at, way])
+                    where = skip if way == 0 else ahead - skip - count
+                    for c in range(2):
+                        narrow(early.at[c, way], where, devs[c][way],
+                               c * half + early_rows(way), count)
+            settle_ring(step, at)
             for way in range(2):
-                if step == 1 and at == 0:
-                    for batch, count in enumerate(EARLY):
-                        settle(q_in.at[:, pl.ds(0, count)], early_sem.at[batch, way])
-                    for c in range(2):
-                        narrow(early.at[c, way], 0, devs[c][way], c * half + early_rows(way), ahead)
-                settle_ring(way, step, at)
-                item = pieces(min(step, steps) if step > 1 else 0, way)[at]
+                item = pieces(step if step > 1 else 0, way)[at]
                 for c in range(2):
                     if step < steps:
                         for later, nxt in enumerate(pieces(step + 1, way)):
                             if item[0] <= nxt[0] < item[0] + item[1]:
                                 ring(c, way, step + 1, later, devs[c][way])
+            for way in range(2):
+                item = pieces(step if step > 1 else 0, way)[at]
                 for c in range(2):
                     pass_on(c, devs[c][way], item)
     settle(line.at[pl.ds(0, len(row_peers)), lines], stat_sem.at[0])
@@ -311,7 +321,7 @@
             dma((4,)),
             dma((2,)),
             dma((2,)),
-            dma((2, steps, 2)),
+            dma((steps, PIECES)),
             dma((2, 2)),
         ],
         compiler_params=pltpu.CompilerParams(

time: 68.4 us -> 68.4 us (level)
  no operation moved by 1% of the time
where the time goes in v6:
time: 68.4 us; the launch traced here: 68.3 us
  Pallas kernels  67.7 us (99%)
    pallas_call x1, Pallas kernels, local(): pl.pallas_call(functools.partial(gather_kernel, ranks, d_model), out_shap...  61.2 us
    pallas_call x1, Pallas kernels, local(): pl.pallas_call(write_kernel, out_shape=shapes, in_specs=[vmem] * 6, out_s...  6.49 us

profile of v6, /device:TPU:1, one launch (start us, length us, event | category | flops | bytes accessed | tf_op | source)
XLA Modules:
  0.0 68.3 jit_solution(13970756868266916745)
XLA Ops:
  0.6 61.2 %shard_map.127 = (bf16[8192,1024]{1,0:T(8,128)(2,1)S(1)}, bf16[64,8192]{1,0:T(8,128)(2,1)S(1)}, bf16[64,8192]{1,0:T(8,128)(2,1)S(1)}, f32[1,1024]{1,0:T(1,128)S(...) custom-call(f32[1,256]{1,0:T(1,128)} %bitcast.15, f32[1,256]{1,0:T(1,128)} %bitcast.16, f32[256,1024]{1,0:T(8,128)} %oq.1, ...), custom_call_target="tpu_custom_call" | custom-call | tf_op jit(solution)/shard_map/pallas_call | solution.py:306
  61.8 6.5 %shard_map.128 = (bf16[8192,1024]{1,0:T(8,128)(2,1)}, bf16[64,8192]{1,0:T(8,128)(2,1)}, bf16[64,8192]{1,0:T(8,128)(2,1)}, f32[1,1024]{1,0:T(1,128)}, f32[1,64]{1,0:T(1,128)}, /*index=5*/f32[1,64]{1,0:T(1,128)}) custom-call(bf16[8192,1024]{1,0:T(8,128)(2,1)S(1)} %get-tuple-element.18.sq, bf16[64,8192]{1,0:T(8,128)(2,1)S(1)} %get-tuple-element.19.sk, ...), custom_call_target="tpu_custom_call" | custom-call | tf_op jit(solution)/shard_map/pallas_call | solution.py:337

commit v7 on v5

--- a/solution.py
+++ b/solution.py
@@ -228,14 +228,6 @@
         for at in range(2):
             for way in range(2):
                 ring(c, way, 1, at, me)
-    for c in range(2):
-        pass_on(c, me, (0, half, 2))
-
-    for j in range(tiles):
-        cq[:, pl.ds(j * 128, 128)] = scale[j:j + 1, :]
-    ck[...] = scale[tiles:tiles + 1, 0:kv_cols]
-    cv[...] = scale[tiles:tiles + 1, kv_cols:2 * kv_cols]
-
     for step in range(1, steps + 1):
         devs = {c: origins(c, step) for c in range(2)}
         for at in range(2):
@@ -254,6 +246,15 @@
                                 ring(c, way, step + 1, later, devs[c][way])
                 for c in range(2):
                     pass_on(c, devs[c][way], item)
+        if step > 1:
+            continue
+        for c in range(2):
+            pass_on(c, me, (0, half, 2))
+
+        for j in range(tiles):
+            cq[:, pl.ds(j * 128, 128)] = scale[j:j + 1, :]
+        ck[...] = scale[tiles:tiles + 1, 0:kv_cols]
+        cv[...] = scale[tiles:tiles + 1, kv_cols:2 * kv_cols]
     settle(line.at[pl.ds(0, len(row_peers)), lines], stat_sem.at[0])
     settle(column.at[pl.ds(0, len(column_peers)), lines], stat_sem.at[2])
     share = half + kv_cols * rows // q_cols

time: 68.4 us -> 68.4 us (level)
  no operation moved by 1% of the time
where the time goes in v7:
time: 68.4 us; the launch traced here: 68.3 us
  Pallas kernels  67.6 us (99%)
    pallas_call x1, Pallas kernels, local(): pl.pallas_call(functools.partial(gather_kernel, ranks, d_model), out_shap...  61.2 us
    pallas_call x1, Pallas kernels, local(): pl.pallas_call(write_kernel, out_shape=shapes, in_specs=[vmem] * 6, out_s...  6.49 us

profile of v7, /device:TPU:1, one launch (start us, length us, event | category | flops | bytes accessed | tf_op | source)
XLA Modules:
  0.0 68.3 jit_solution(2583143928631881407)
XLA Ops:
  0.6 61.2 %shard_map.127 = (bf16[8192,1024]{1,0:T(8,128)(2,1)S(1)}, bf16[64,8192]{1,0:T(8,128)(2,1)S(1)}, bf16[64,8192]{1,0:T(8,128)(2,1)S(1)}, f32[1,1024]{1,0:T(1,128)S(...) custom-call(f32[1,256]{1,0:T(1,128)} %bitcast.15, f32[1,256]{1,0:T(1,128)} %bitcast.16, f32[256,1024]{1,0:T(8,128)} %oq.1, ...), custom_call_target="tpu_custom_call" | custom-call | tf_op jit(solution)/shard_map/pallas_call | solution.py:297
  61.8 6.5 %shard_map.128 = (bf16[8192,1024]{1,0:T(8,128)(2,1)}, bf16[64,8192]{1,0:T(8,128)(2,1)}, bf16[64,8192]{1,0:T(8,128)(2,1)}, f32[1,1024]{1,0:T(1,128)}, f32[1,64]{1,0:T(1,128)}, /*index=5*/f32[1,64]{1,0:T(1,128)}) custom-call(bf16[8192,1024]{1,0:T(8,128)(2,1)S(1)} %get-tuple-element.18.sq, bf16[64,8192]{1,0:T(8,128)(2,1)S(1)} %get-tuple-element.19.sk, ...), custom_call_target="tpu_custom_call" | custom-call | tf_op jit(solution)/shard_map/pallas_call | solution.py:328
